TPU v7x, 32 devices: a whole 2x2x4 slice. The times are simulated.
32 devices in a mesh: dp: 16 (over z, y, x), layer: 2 (over core).
Axes of the slice: x: 2, y: 2, z: 4, core: 2. Of those that a mesh axis runs over, the one named last changes fastest.
Arguments:
- layer_inputs: bfloat16 [2, 16384, 4096], P('layer', 'dp'), may hold values from -6 to 6
- output_grads: bfloat16 [2, 16384, 512], P('layer', 'dp'), may hold values from -6 to 6
- input_factors: bfloat16 [128, 2, 4, 4096], P('dp', 'layer'), may hold values from -0.09375 to 0.09375
- output_factors: bfloat16 [128, 2, 4, 512], P('dp', 'layer'), may hold values from -0.25 to 0.25
Outputs:
- scores: float32 [128, 16384], P(None, 'dp')
All inputs are finite; a program needn't handle non-finite values.
Results may differ from a plain program's by a relative error of at most 0.0003.
Values may be sent and summed in bfloat16 or wider, within the bound.
A program may use at most 128 MiB of HBM per device.

v0:
```python
import functools

import jax
import jax.numpy as jnp
from jax import lax
from jax.experimental import pallas as pl
from jax.experimental.pallas import tpu as pltpu
from jax.sharding import PartitionSpec as P

MESH = pl.DeviceIdType.MESH
OWN, ACROSS_X, ACROSS_Y, DIAG = range(4)
PIECES = 2


def kernel(nz, layers, count, rank, own_ref, acts_hbm, grads_hbm, out_ref,
           slots, acts, grads, parts, load_sem, recv_sem, x_sem, y_sem, z_sem, psend_sem, precv_sem):
    me = lax.axis_index("dp")
    layer = lax.axis_index("layer")
    x, y, z = me % 2, (me // 2) % 2, me // 4
    rows, width = own_ref.shape
    half = rows // PIECES
    d_in = acts.shape[1]
    tokens = acts.shape[0]
    to_x = {"dp": me + 1 - 2 * x}
    to_y = {"dp": me + 2 - 4 * y}
    to_up = {"dp": (me + 4) % (4 * nz)}
    to_down = {"dp": (me + 4 * nz - 4) % (4 * nz)}
    has_up, has_down = z < nz - 1, z > 0

    load_acts = pltpu.make_async_copy(acts_hbm, acts, load_sem.at[0])
    load_grads = pltpu.make_async_copy(grads_hbm, grads, load_sem.at[1])
    load_acts.start()
    load_grads.start()

    barrier = pltpu.get_barrier_semaphore()
    pl.semaphore_signal(barrier, inc=1, device_id=to_x, device_id_type=MESH)
    pl.semaphore_signal(barrier, inc=1, device_id=to_y, device_id_type=MESH)
    for k in range(1, layers):
        pl.semaphore_signal(barrier, inc=1, device_id={"layer": (layer + k) % layers}, device_id_type=MESH)

    @pl.when(has_up)
    def _():
        pl.semaphore_signal(barrier, inc=1, device_id=to_up, device_id_type=MESH)

    @pl.when(has_down)
    def _():
        pl.semaphore_signal(barrier, inc=1, device_id=to_down, device_id_type=MESH)

    line_ends = (z + nz - 2) // (nz - 1) + (2 * nz - 3 - z) // (nz - 1)
    pl.semaphore_wait(barrier, 2 + layers - 1 + line_ends)

    def copy(src, target, level, piece, sem, device):
        at = target * nz + level
        return pltpu.make_async_remote_copy(
            src_ref=src,
            dst_ref=slots.at[at, pl.ds(piece * half, half), :],
            send_sem=sem,
            recv_sem=recv_sem.at[at, piece],
            device_id=device,
            device_id_type=MESH,
        )

    def held(source, level, piece):
        return slots.at[source * nz + level, pl.ds(piece * half, half), :]

    def arrived(target, level, piece):
        copy(held(target, level, piece), target, level, piece, x_sem.at[0, 0, 0], to_x).wait_recv()

    def mine(level, piece, first):
        return own_ref.at[pl.ds(piece * half, half), :] if first else held(OWN, level, piece)

    def up(level, piece, first):
        return copy(mine(level, piece, first), OWN, level, piece, z_sem.at[0, level, piece], to_up)

    def down(level, piece, first):
        return copy(mine(level, piece, first), OWN, level, piece, z_sem.at[1, level, piece], to_down)

    def side_x(level, piece, first):
        return copy(mine(level, piece, first), ACROSS_X, level, piece, x_sem.at[0, level, piece], to_x)

    def side_y(level, piece, first):
        return copy(mine(level, piece, first), ACROSS_Y, level, piece, y_sem.at[0, level, piece], to_y)

    def turn_x(level):
        return copy(held(ACROSS_Y, level, 0), DIAG, level, 0, x_sem.at[1, level, 0], to_x)

    def turn_y(level):
        return copy(held(ACROSS_X, level, 1), DIAG, level, 1, y_sem.at[1, level, 1], to_y)

    def at_distance(step, act):
        if step == 0:
            act(z, None)
            return

        @pl.when(z >= step)
        def _():
            act(z - step, True)

        @pl.when(z + step < nz)
        def _():
            act(z + step, False)

    def turn(level, unused):
        arrived(ACROSS_Y, level, 0)
        turn_x(level).start()
        arrived(ACROSS_X, level, 1)
        turn_y(level).start()

    for piece in range(PIECES):
        @pl.when(has_up)
        def _():
            up(z, piece, True).start()

        @pl.when(has_down)
        def _():
            down(z, piece, True).start()

        side_x(z, piece, True).start()
        side_y(z, piece, True).start()
    slots[OWN * nz + z] = own_ref[...]

    for step in range(1, nz):
        for piece in range(PIECES):
            def relay(level, from_below):
                arrived(OWN, level, piece)
                if from_below:
                    @pl.when(has_up)
                    def _():
                        up(level, piece, False).start()
                else:
                    @pl.when(has_down)
                    def _():
                        down(level, piece, False).start()
                side_x(level, piece, False).start()
                side_y(level, piece, False).start()

            at_distance(step, relay)
        at_distance(step - 1, turn)
    at_distance(nz - 1, turn)

    chunk = min(256, tokens)

    def scores_of(first, classes):
        blocks = classes * nz

        def body(i, carry):
            cols = pl.ds(pl.multiple_of(i * chunk, chunk), chunk)
            left = slots[first * nz:first * nz + blocks]
            left = left.reshape(blocks * rows, width)
            dims = (((1,), (1,)), ((), ()))
            proj_in = lax.dot_general(left[:, :d_in], acts[cols, :], dims, preferred_element_type=jnp.float32)
            proj_out = lax.dot_general(left[:, d_in:], grads[cols, :], dims, preferred_element_type=jnp.float32)
            joined = (proj_in * proj_out).reshape(blocks, rank, count, chunk)
            term = jnp.sum(joined, axis=1).reshape(blocks * count, chunk)
            parts[layer, first * nz * count:(first * nz + blocks) * count, cols] = term
            return carry

        lax.fori_loop(0, tokens // chunk, body, 0)

    def share(stage, first, classes, k):
        span = pl.ds(first * nz * count, classes * nz * count)
        return pltpu.make_async_remote_copy(
            src_ref=parts.at[layer, span, :],
            dst_ref=parts.at[layer, span, :],
            send_sem=psend_sem.at[stage, k],
            recv_sem=precv_sem.at[stage, layer],
            device_id={"layer": (layer + k) % layers},
            device_id_type=MESH,
        )

    def shared(stage, first, classes, k):
        source = (layer + k) % layers
        span = pl.ds(first * nz * count, classes * nz * count)
        pltpu.make_async_remote_copy(
            src_ref=parts.at[source, span, :],
            dst_ref=parts.at[source, span, :],
            send_sem=psend_sem.at[stage, k],
            recv_sem=precv_sem.at[stage, source],
            device_id={"layer": source},
            device_id_type=MESH,
        ).wait_recv()

    def finish(first, classes):
        for kind in range(first, first + classes):
            col = ((1 - y) if kind in (ACROSS_Y, DIAG) else y) * 2
            col = col + ((1 - x) if kind in (ACROSS_X, DIAG) else x)
            for level in range(nz):
                at = (kind * nz + level) * count
                total = parts[0, at:at + count, :]
                for other in range(1, layers):
                    total = total + parts[other, at:at + count, :]
                out_ref[pl.ds(pl.multiple_of((level * 4 + col) * count, count), count), :] = total

    for step in range(nz):
        def rest(level, unused):
            arrived(ACROSS_X, level, 0)
            arrived(ACROSS_Y, level, 1)

        at_distance(step, rest)
    load_acts.wait()
    load_grads.wait()
    scores_of(OWN, 3)
    for k in range(1, layers):
        share(0, OWN, 3, k).start()

    for step in range(nz):
        def last(level, unused):
            arrived(DIAG, level, 0)
            arrived(DIAG, level, 1)

        at_distance(step, last)
    scores_of(DIAG, 1)
    for k in range(1, layers):
        shared(0, OWN, 3, k)
    finish(OWN, 3)
    for k in range(1, layers):
        share(1, DIAG, 1, k).start()
    for k in range(1, layers):
        shared(1, DIAG, 1, k)
    finish(DIAG, 1)

    for step in range(nz):
        def sent(level, from_below):
            for piece in range(PIECES):
                if from_below is not False:
                    @pl.when(has_up)
                    def _():
                        up(level, piece, step == 0).wait_send()
                if from_below is not True:
                    @pl.when(has_down)
                    def _():
                        down(level, piece, step == 0).wait_send()
                side_x(level, piece, step == 0).wait_send()
                side_y(level, piece, step == 0).wait_send()
            turn_x(level).wait_send()
            turn_y(level).wait_send()

        at_distance(step, sent)
    for k in range(1, layers):
        share(0, OWN, 3, k).wait_send()
        share(1, DIAG, 1, k).wait_send()


def shards(nz, layers, layer_inputs, output_grads, input_factors, output_factors):
    count, _, rank, d_in = input_factors.shape
    d_out = output_factors.shape[3]
    tokens = layer_inputs.shape[1]
    rows, width = count * rank, d_in + d_out
    own = jnp.concatenate([input_factors[:, 0], output_factors[:, 0]], axis=2)
    own = jnp.swapaxes(own, 0, 1).reshape(rows, width)
    queries = 4 * nz * count
    dma = pltpu.SemaphoreType.DMA
    return pl.pallas_call(
        functools.partial(kernel, nz, layers, count, rank),
        out_shape=jax.ShapeDtypeStruct((queries, tokens), jnp.float32),
        in_specs=[
            pl.BlockSpec(memory_space=pltpu.VMEM),
            pl.BlockSpec(memory_space=pl.ANY),
            pl.BlockSpec(memory_space=pl.ANY),
        ],
        out_specs=pl.BlockSpec(memory_space=pltpu.VMEM),
        scratch_shapes=[
            pltpu.VMEM((4 * nz, rows, width), jnp.bfloat16),
            pltpu.VMEM((tokens, d_in), jnp.bfloat16),
            pltpu.VMEM((tokens, d_out), jnp.bfloat16),
            pltpu.VMEM((layers, queries, tokens), jnp.float32),
            dma((2,)),
            dma((4 * nz, PIECES)),
            dma((2, nz, PIECES)),
            dma((2, nz, PIECES)),
            dma((2, nz, PIECES)),
            dma((2, layers)),
            dma((2, layers)),
        ],
        compiler_params=pltpu.CompilerParams(
            collective_id=0, has_side_effects=True, vmem_limit_bytes=60 * 1024 * 1024
        ),
    )(own, layer_inputs[0], output_grads[0])


def solution(mesh):
    in_specs = (
        P("layer", "dp", None),
        P("layer", "dp", None),
        P("dp", "layer", None, None),
        P("dp", "layer", None, None),
    )
    body = functools.partial(shards, mesh.shape["dp"] // 4, mesh.shape["layer"])
    return jax.shard_map(body, mesh=mesh, in_specs=in_specs, out_specs=P(None, "dp"), check_vma=False)
```

profile of v0, /device:TPU:0, one launch (start us, length us, event | category | flops | bytes accessed | tf_op | source)
XLA Modules:
  0.0 53.8 jit_solution(13718313518883708312)
XLA Ops:
  0.0 1.1 %maximum_bitcast_fusion = bf16[4,8,4608]{2,0,1:T(4,128)(2,1)S(1)} fusion(bf16[8,4,512]{2,1,0:T(4,128)(2,1)} %bitcast.13, bf16[8,4,4096]{2,1,0:T(4,128)(2,1)} %bitcast.12), kind=kLoop, calls=%fused_computation | loop fusion | flops 589824 | bytes 589824 | tf_op jit(solution)/shard_map/transpose | solution.py:250
  1.1 0.8 %copy.7 = bf16[4,8,4608]{2,1,0:T(8,128)(2,1)} copy(bf16[4,8,4608]{2,0,1:T(4,128)(2,1)S(1)} %maximum_bitcast_fusion) | data formatting | bytes 589824 | tf_op jit(solution)/shard_map/transpose | solution.py:250
  1.9 50.1 %shard_map.46 = f32[128,1024]{1,0:T(8,128)} custom-call(bf16[32,4608]{1,0:T(8,128)(2,1)} %bitcast.10, bf16[1024,4096]{1,0:T(8,128)(2,1)} %bitcast.9, bf16[1024,512]{1,0:T(8,128)(2,1)} %bitcast.11), custom_call_target="tpu_custom_call" | custom-call | tf_op jit(solution)/shard_map/pallas_call | solution.py:253
  52.0 1.9 %copy.9 = f32[128,1024]{1,0:T(8,128)} copy(f32[128,1024]{1,0:T(8,128)} %shard_map.46) | data formatting | bytes 1048576
where the time goes:
time: 54.1 us; the launch traced here: 53.8 us
  Pallas kernels  50.1 us (93%)
  local copies, waits for them, and re-layouts  2.65 us (5%)
  other arithmetic  1.1 us (2%)
    pallas_call x1, Pallas kernels, shards(): pl.pallas_call(functools.partial(kernel, nz, layers, count, rank), out_sh...  50.1 us
    unnamed x1, local copies, waits for them, and re-layouts  1.89 us
    transpose x1, other arithmetic, shards(): own = jnp.swapaxes(own, 0, 1).reshape(rows, width)  1.1 us

commit v1 on v0

v1 whole, which is shorter than its diff:
```python
import functools

import jax
import jax.numpy as jnp
from jax import lax
from jax.experimental import pallas as pl
from jax.experimental.pallas import tpu as pltpu
from jax.sharding import PartitionSpec as P

MESH = pl.DeviceIdType.MESH
OWN, ACROSS_X, ACROSS_Y, DIAG = range(4)
LINKS = ("x", "y", "in", "ex")
CUTS = 4
BATCH = 4
AHEAD = 2
LATENCY = 1.6
RATE = 730.0
COMPUTE = 0.8
TUNED = {
    4: {
        (0, "x"): ((ACROSS_Y, 0), (OWN, 2), (OWN, 0), (ACROSS_Y, 2), (OWN, 1), (OWN, 3)),
        (0, "in"): ((OWN, 0), (DIAG, 2), (DIAG, 0)),
        (1, "x"): ((ACROSS_Y, 1), (OWN, 3), (OWN, 1), (OWN, 0), (ACROSS_Y, 3), (OWN, 2)),
        (1, "in"): ((OWN, 1), (OWN, 0)),
        (1, "ex"): ((OWN, 2), (OWN, 3), (DIAG, 1), (OWN, 1), (DIAG, 3)),
    }
}


def rank_of(nz, end, link, kind, level, piece):
    if link == "y":
        link, kind = "x", {ACROSS_X: ACROSS_Y}.get(kind, kind)
    if nz in TUNED:
        return TUNED[nz][end, link].index((kind, level)), piece
    away = abs(level - end)
    if link == "x":
        return away + (0.5 if kind != OWN else 0.0), piece
    return away + (1.5 if kind != OWN else 0.0), piece


def receiver(half, nz, end, link, level):
    if link in ("x", "y"):
        return end, level
    if link == "ex":
        return end - 1, level
    return (end + 1, level) if end + 1 < half else (end, nz - 1 - level)


def simulate(nz, widths):
    half, pieces = nz // 2, range(len(widths))
    todo, avail = {}, {}
    for end in range(half):
        queue = {link: [] for link in LINKS}
        for level in range(nz):
            for piece in pieces:
                queue["x"].append((OWN, level, piece, ACROSS_X))
                queue["y"].append((OWN, level, piece, ACROSS_Y))
                if level % 2 == end % 2:
                    if (level // 2 + piece) % 2 == 0:
                        queue["x"].append((ACROSS_Y, level, piece, DIAG))
                    else:
                        queue["y"].append((ACROSS_X, level, piece, DIAG))
                    queue["in" if end % 2 == 0 else "ex"].append((DIAG, level, piece, DIAG))
                if level <= end:
                    queue["in"].append((OWN, level, piece, OWN))
                if level >= end > 0:
                    queue["ex"].append((OWN, level, piece, OWN))
        for piece in pieces:
            avail[end, OWN, end, piece] = 0.0
        todo.update({(end, link): items for link, items in queue.items() if items})
    free = {key: 0.0 for key in todo}
    sent = {key: [] for key in todo}
    while any(todo.values()):
        best = None
        for key, items in todo.items():
            for item in items:
                start = max(free[key], avail.get((key[0], *item[:3]), 1e9))
                if best is None or start < best[0] - 1e-9:
                    best = (start, key, [])
                if best[1] == key and start <= best[0] + 1e-9:
                    best[2].append(item)
        start, (end, link), ready = best
        item = min(ready, key=lambda it: rank_of(nz, end, link, *it[:3]))
        todo[end, link].remove(item)
        free[end, link] = start + widths[item[2]] / RATE
        there, level = receiver(half, nz, end, link, item[1])
        avail[there, item[3], level, item[2]] = free[end, link] + LATENCY
        sent[end, link].append((start, item))
    return sent, avail


def plan(nz, widths):
    half, pieces = nz // 2, len(widths)
    sent, avail = simulate(nz, widths)
    slot = {}
    for end in range(half):
        shares = [(kind, level) for kind in range(4) for level in range(nz)]
        shares.sort(key=lambda s: (s != (OWN, end), max(avail[end, *s, p] for p in range(pieces))))
        slot[end] = {share: at for at, share in enumerate(shares)}
    steps = [(batch, piece) for batch in range(4 * nz // BATCH) for piece in range(pieces)]
    events = {}
    for end in range(half):
        found = []
        for (sender, link), items in sent.items():
            if sender != end:
                continue
            for i, (start, (kind, level, piece, arrives)) in enumerate(items):
                at = max(avail[end, kind, level, piece], items[i - AHEAD][0] if i >= AHEAD else 0.0)
                there, counted = receiver(half, nz, end, link, level)
                found.append((at, 0, len(found), ("send", link, i, slot[end][kind, level], slot[there][arrives, counted], piece)))
        order = sorted(found)
        events[end], clock, done = [], 0.0, 0
        members = {}
        for share, at in slot[end].items():
            members.setdefault(at // BATCH, []).append((share, at))
        for batch, piece in steps:
            need = [(avail[end, *share, piece], at) for share, at in members[batch]]
            clock = max([clock] + [t for t, _ in need])
            part = []
            while done < len(order) and order[done][0] <= clock:
                part.append(order[done])
                done += 1
            part += [(t, 1, at, ("wait", at, piece)) for t, at in need]
            events[end].append([event for *_, event in sorted(part)])
            clock += COMPUTE * widths[piece] / 1024
        events[end].append([event for *_, event in order[done:]])
    return slot, steps, events


def kernel(nz, layers, count, rank, widths, in_hbm, ofac_hbm, acts_hbm, grads_hbm, out_ref,
           raw_in, raw_out, slots_in, slots_out, acts, grads, total, parts,
           load_sem, recv_sem, send_sem, psend_sem, precv_sem):
    me = lax.axis_index("dp")
    layer = lax.axis_index("layer")
    x, y, z = me % 2, (me // 2) % 2, me // 4
    half = nz // 2
    rows = count * rank
    tokens = acts.shape[0]
    cut = slots_in.shape[2]
    low = z < half
    end = jnp.where(low, z, nz - 1 - z)
    inward = jnp.where(low, 4, 4 * nz - 4)
    target = {
        "x": {"dp": me + 1 - 2 * x},
        "y": {"dp": me + 2 - 4 * y},
        "in": {"dp": (me + inward) % (4 * nz)},
        "ex": {"dp": (me + 4 * nz - inward) % (4 * nz)},
    }
    slot, steps, events = plan(nz, widths)

    load_in = pltpu.make_async_copy(in_hbm, raw_in, load_sem.at[0])
    load_out = pltpu.make_async_copy(ofac_hbm, raw_out, load_sem.at[1])
    load_acts = pltpu.make_async_copy(acts_hbm, acts, load_sem.at[2])
    load_grads = pltpu.make_async_copy(grads_hbm, grads, load_sem.at[3])
    load_in.start()
    load_out.start()
    load_acts.start()
    load_grads.start()

    barrier = pltpu.get_barrier_semaphore()
    for link in ("x", "y", "in"):
        pl.semaphore_signal(barrier, inc=1, device_id=target[link], device_id_type=MESH)
    for k in range(1, layers):
        pl.semaphore_signal(barrier, inc=1, device_id={"layer": (layer + k) % layers}, device_id_type=MESH)

    @pl.when(end > 0)
    def _():
        pl.semaphore_signal(barrier, inc=1, device_id=target["ex"], device_id_type=MESH)

    load_in.wait()
    load_out.wait()
    for piece in range(len(widths) - 1):
        own = jnp.swapaxes(raw_in[:, :, piece * cut:(piece + 1) * cut], 0, 1).reshape(rows, cut)
        slots_in[piece, :rows, :] = own
    slots_out[:rows, :] = jnp.swapaxes(raw_out[...], 0, 1).reshape(rows, slots_out.shape[1])
    pl.semaphore_wait(barrier, 3 + layers - 1 + jnp.where(end > 0, 1, 0))

    def held(at, piece):
        span = pl.ds(at * rows, rows)
        return slots_in.at[piece, span, :] if piece < len(widths) - 1 else slots_out.at[span, :]

    def send(link, i, source, dest, piece):
        return pltpu.make_async_remote_copy(
            src_ref=held(source, piece),
            dst_ref=held(dest, piece),
            send_sem=send_sem.at[LINKS.index(link), i],
            recv_sem=recv_sem.at[dest, piece],
            device_id=target[link],
            device_id_type=MESH,
        )

    def arrived(at, piece):
        pltpu.make_async_remote_copy(
            src_ref=held(at, piece),
            dst_ref=held(at, piece),
            send_sem=send_sem.at[0, 0],
            recv_sem=recv_sem.at[at, piece],
            device_id=target["x"],
            device_id_type=MESH,
        ).wait_recv()

    seen = {k: {(0, piece) for piece in range(len(widths))} for k in range(half)}

    def communicate(step):
        for k in range(half):
            def act(k=k):
                for what, *args in events[k][step]:
                    source, piece = (args[2], args[4]) if what == "send" else args
                    if (source, piece) not in seen[k]:
                        seen[k].add((source, piece))
                        arrived(source, piece)
                    if what == "send":
                        send(*args).start()

            if events[k][step]:
                pl.when(end == k)(act)

    chunk = min(256, tokens)
    group = BATCH * rows
    dims = (((1,), (1,)), ((), ()))

    def multiply(batch, piece):
        def body(i, carry):
            cols = pl.ds(pl.multiple_of(i * chunk, chunk), chunk)
            span = slice(batch * group, (batch + 1) * group)
            if piece < len(widths) - 1:
                left, right = slots_in[piece, span, :], acts[cols, piece * cut:(piece + 1) * cut]
                term = lax.dot_general(left, right, dims, preferred_element_type=jnp.float32)
                total[:, cols] = term if piece == 0 else total[:, cols] + term
            else:
                proj_out = lax.dot_general(slots_out[span, :], grads[cols, :], dims, preferred_element_type=jnp.float32)
                joined = (total[:, cols] * proj_out).reshape(BATCH, rank, count, chunk)
                parts[layer, batch, :, cols] = jnp.sum(joined, axis=1).reshape(BATCH * count, chunk)
            return carry

        lax.fori_loop(0, tokens // chunk, body, 0)

    def share(batch, k, to):
        return pltpu.make_async_remote_copy(
            src_ref=parts.at[to, batch],
            dst_ref=parts.at[to, batch],
            send_sem=psend_sem.at[batch, k],
            recv_sem=precv_sem.at[batch, to],
            device_id={"layer": (layer + k) % layers},
            device_id_type=MESH,
        )

    def finish(batch):
        for k in range(1, layers):
            share(batch, k, (layer + k) % layers).wait_recv()
        for i in range(BATCH):
            base = 0
            for k in range(half):
                kind, level = [share for share, at in slot[k].items() if at == batch * BATCH + i][0]
                col = ((1 - y) if kind in (ACROSS_Y, DIAG) else y) * 2 + ((1 - x) if kind in (ACROSS_X, DIAG) else x)
                at = jnp.where(low, level, nz - 1 - level) * 4 + col
                base = base + jnp.where(end == k, at, 0)
            score = parts[0, batch, i * count:(i + 1) * count, :]
            for other in range(1, layers):
                score = score + parts[other, batch, i * count:(i + 1) * count, :]
            out_ref[pl.ds(pl.multiple_of(base * count, count), count), :] = score

    for step, (batch, piece) in enumerate(steps):
        communicate(step)
        if step == 0:
            load_acts.wait()
            load_grads.wait()
        multiply(batch, piece)
        if piece == 0 and batch > 0:
            finish(batch - 1)
        if piece == len(widths) - 1:
            for k in range(1, layers):
                share(batch, k, layer).start()
    communicate(len(steps))
    finish(steps[-1][0])

    for k in range(half):
        def sent(k=k):
            for what, *args in sum(events[k], []):
                if what == "send":
                    send(*args).wait_send()

        pl.when(end == k)(sent)
    for batch in range(steps[-1][0] + 1):
        for k in range(1, layers):
            share(batch, k, layer).wait_send()


def shards(nz, layers, layer_inputs, output_grads, input_factors, output_factors):
    count, _, rank, d_in = input_factors.shape
    d_out = output_factors.shape[3]
    tokens = layer_inputs.shape[1]
    rows, cut = count * rank, d_in // CUTS
    widths = (cut,) * CUTS + (d_out,)
    slots = 4 * nz
    queue = max(len(items) for items in simulate(nz, widths)[0].values())
    dma = pltpu.SemaphoreType.DMA
    return pl.pallas_call(
        functools.partial(kernel, nz, layers, count, rank, widths),
        out_shape=jax.ShapeDtypeStruct((slots * count, tokens), jnp.float32),
        in_specs=[pl.BlockSpec(memory_space=pl.ANY)] * 4,
        out_specs=pl.BlockSpec(memory_space=pltpu.VMEM),
        scratch_shapes=[
            pltpu.VMEM((count, rank, d_in), jnp.bfloat16),
            pltpu.VMEM((count, rank, d_out), jnp.bfloat16),
            pltpu.VMEM((CUTS, slots * rows, cut), jnp.bfloat16),
            pltpu.VMEM((slots * rows, d_out), jnp.bfloat16),
            pltpu.VMEM((tokens, d_in), jnp.bfloat16),
            pltpu.VMEM((tokens, d_out), jnp.bfloat16),
            pltpu.VMEM((BATCH * rows, tokens), jnp.float32),
            pltpu.VMEM((layers, slots // BATCH, BATCH * count, tokens), jnp.float32),
            dma((4,)),
            dma((slots, CUTS + 1)),
            dma((4, queue)),
            dma((slots // BATCH, layers)),
            dma((slots // BATCH, layers)),
        ],
        compiler_params=pltpu.CompilerParams(
            collective_id=0, has_side_effects=True, vmem_limit_bytes=60 * 1024 * 1024
        ),
    )(input_factors[:, 0], output_factors[:, 0], layer_inputs[0], output_grads[0])


def solution(mesh):
    in_specs = (
        P("layer", "dp", None),
        P("layer", "dp", None),
        P("dp", "layer", None, None),
        P("dp", "layer", None, None),
    )
    body = functools.partial(shards, mesh.shape["dp"] // 4, mesh.shape["layer"])
    return jax.shard_map(body, mesh=mesh, in_specs=in_specs, out_specs=P(None, "dp"), check_vma=False)
```

time: 54.1 us -> 51.4 us (0.950)
  other arithmetic: 1.1 us -> 0 us
  local copies, waits for them, and re-layouts: 2.65 us -> 1.89 us
  Pallas kernels: 50.1 us -> 49.4 us
    transpose x1 -> x0, other arithmetic: 1.1 us -> none  [shards(): own = jnp.swapaxes(own, 0, 1).reshape(rows, width)]
    transpose x1 -> x0, local copies, waits for them, and re-layouts: 0.76 us -> none  [shards(): own = jnp.swapaxes(own, 0, 1).reshape(rows, width)]
    pallas_call x1, Pallas kernels: 50.1 us -> 49.4 us  [shards(): pl.pallas_call(functools.partial(kernel, nz, layers, count, rank, widths)...]
where the time goes in v1:
time: 51.4 us; the launch traced here: 51.3 us
  Pallas kernels  49.4 us (96%)
  local copies, waits for them, and re-layouts  1.89 us (4%)
    pallas_call x1, Pallas kernels, shards(): pl.pallas_call(functools.partial(kernel, nz, layers, count, rank, widths)...  49.4 us
    unnamed x1, local copies, waits for them, and re-layouts  1.89 us

profile of v1, /device:TPU:0, one launch (start us, length us, event | category | flops | bytes accessed | tf_op | source)
XLA Modules:
  0.0 51.3 jit_solution(1927592867020468285)
XLA Ops:
  0.0 49.4 %shard_map.46 = f32[128,1024]{1,0:T(8,128)} custom-call(bf16[8,4,4096]{2,1,0:T(4,128)(2,1)} %bitcast.6, bf16[8,4,512]{2,1,0:T(4,128)(2,1)} %bitcast.7, bf16[1024,4096]{1,0:T(8,128)(2,1)} %bitcast.4, bf16[1024,512]{1,0:T(8,128)(2,1)} %bitcast.5), custom_call_target="tpu_custom_call" | custom-call | tf_op jit(solution)/shard_map/pallas_call | solution.py:298
  49.4 1.9 %copy.6 = f32[128,1024]{1,0:T(8,128)} copy(f32[128,1024]{1,0:T(8,128)} %shard_map.46) | data formatting | bytes 1048576

commit v2 on v1

--- a/solution.py
+++ b/solution.py
@@ -10,7 +10,7 @@
 MESH = pl.DeviceIdType.MESH
 OWN, ACROSS_X, ACROSS_Y, DIAG = range(4)
 LINKS = ("x", "y", "in", "ex")
-CUTS = 4
+CUTS = 2
 BATCH = 4
 AHEAD = 2
 LATENCY = 1.6
@@ -104,8 +104,9 @@
         for (sender, link), items in sent.items():
             if sender != end:
                 continue
+            at = 0.0
             for i, (start, (kind, level, piece, arrives)) in enumerate(items):
-                at = max(avail[end, kind, level, piece], items[i - AHEAD][0] if i >= AHEAD else 0.0)
+                at = max(at, avail[end, kind, level, piece], items[i - AHEAD][0] if i >= AHEAD else 0.0)
                 there, counted = receiver(half, nz, end, link, level)
                 found.append((at, 0, len(found), ("send", link, i, slot[end][kind, level], slot[there][arrives, counted], piece)))
         order = sorted(found)
@@ -215,7 +216,7 @@
             if events[k][step]:
                 pl.when(end == k)(act)
 
-    chunk = min(256, tokens)
+    chunk = min(1024, tokens)
     group = BATCH * rows
     dims = (((1,), (1,)), ((), ()))
 

time: 51.4 us -> 43.9 us (0.85)
  Pallas kernels: 49.4 us -> 41.9 us
    pallas_call x1, Pallas kernels: 49.4 us -> 41.9 us  [shards(): pl.pallas_call(functools.partial(kernel, nz, layers, count, rank, widths)...]
where the time goes in v2:
time: 43.9 us; the launch traced here: 43.8 us
  Pallas kernels  41.9 us (95%)
  local copies, waits for them, and re-layouts  1.89 us (4%)
    pallas_call x1, Pallas kernels, shards(): pl.pallas_call(functools.partial(kernel, nz, layers, count, rank, widths)...  41.9 us
    unnamed x1, local copies, waits for them, and re-layouts  1.89 us

profile of v2, /device:TPU:0, one launch (start us, length us, event | category | flops | bytes accessed | tf_op | source)
XLA Modules:
  0.0 43.8 jit_solution(7679408588630707378)
XLA Ops:
  0.0 41.9 %shard_map.46 = f32[128,1024]{1,0:T(8,128)} custom-call(bf16[8,4,4096]{2,1,0:T(4,128)(2,1)} %bitcast.6, bf16[8,4,512]{2,1,0:T(4,128)(2,1)} %bitcast.7, bf16[1024,4096]{1,0:T(8,128)(2,1)} %bitcast.4, bf16[1024,512]{1,0:T(8,128)(2,1)} %bitcast.5), custom_call_target="tpu_custom_call" | custom-call | tf_op jit(solution)/shard_map/pallas_call | solution.py:299
  41.9 1.9 %copy.6 = f32[128,1024]{1,0:T(8,128)} copy(f32[128,1024]{1,0:T(8,128)} %shard_map.46) | data formatting | bytes 1048576

commit v3 on v2

--- a/solution.py
+++ b/solution.py
@@ -11,11 +11,14 @@
 OWN, ACROSS_X, ACROSS_Y, DIAG = range(4)
 LINKS = ("x", "y", "in", "ex")
 CUTS = 2
+LIMIT = 48
 BATCH = 4
 AHEAD = 2
 LATENCY = 1.6
 RATE = 730.0
-COMPUTE = 0.8
+COMPUTE = 0.5
+TURN = 0.9
+BEGIN = 2.5
 TUNED = {
     4: {
         (0, "x"): ((ACROSS_Y, 0), (OWN, 2), (OWN, 0), (ACROSS_Y, 2), (OWN, 1), (OWN, 3)),
@@ -97,7 +100,8 @@
         shares = [(kind, level) for kind in range(4) for level in range(nz)]
         shares.sort(key=lambda s: (s != (OWN, end), max(avail[end, *s, p] for p in range(pieces))))
         slot[end] = {share: at for at, share in enumerate(shares)}
-    steps = [(batch, piece) for batch in range(4 * nz // BATCH) for piece in range(pieces)]
+    steps = [(None, piece) for piece in range(pieces)]
+    steps += [(batch, piece) for batch in range(4 * nz // BATCH) for piece in range(pieces)]
     events = {}
     for end in range(half):
         found = []
@@ -110,12 +114,12 @@
                 there, counted = receiver(half, nz, end, link, level)
                 found.append((at, 0, len(found), ("send", link, i, slot[end][kind, level], slot[there][arrives, counted], piece)))
         order = sorted(found)
-        events[end], clock, done = [], 0.0, 0
+        events[end], clock, done = [], BEGIN, 0
         members = {}
         for share, at in slot[end].items():
             members.setdefault(at // BATCH, []).append((share, at))
         for batch, piece in steps:
-            need = [(avail[end, *share, piece], at) for share, at in members[batch]]
+            need = [(avail[end, *share, piece], at) for share, at in members.get(batch, [])]
             clock = max([clock] + [t for t, _ in need])
             part = []
             while done < len(order) and order[done][0] <= clock:
@@ -123,13 +127,13 @@
                 done += 1
             part += [(t, 1, at, ("wait", at, piece)) for t, at in need]
             events[end].append([event for *_, event in sorted(part)])
-            clock += COMPUTE * widths[piece] / 1024
+            clock += (TURN if batch is None else COMPUTE) * widths[piece] / 1024
         events[end].append([event for *_, event in order[done:]])
     return slot, steps, events
 
 
 def kernel(nz, layers, count, rank, widths, in_hbm, ofac_hbm, acts_hbm, grads_hbm, out_ref,
-           raw_in, raw_out, slots_in, slots_out, acts, grads, total, parts,
+           raw_in, raw_out, slots_in, slots_out, acts, grads, acts_t, grads_t, total, parts,
            load_sem, recv_sem, send_sem, psend_sem, precv_sem):
     me = lax.axis_index("dp")
     layer = lax.axis_index("layer")
@@ -151,12 +155,17 @@
 
     load_in = pltpu.make_async_copy(in_hbm, raw_in, load_sem.at[0])
     load_out = pltpu.make_async_copy(ofac_hbm, raw_out, load_sem.at[1])
-    load_acts = pltpu.make_async_copy(acts_hbm, acts, load_sem.at[2])
-    load_grads = pltpu.make_async_copy(grads_hbm, grads, load_sem.at[3])
     load_in.start()
     load_out.start()
-    load_acts.start()
-    load_grads.start()
+
+    def load(piece):
+        if piece == len(widths) - 1:
+            return pltpu.make_async_copy(grads_hbm, grads, load_sem.at[2 + piece])
+        span = pl.ds(piece * cut, cut)
+        return pltpu.make_async_copy(acts_hbm.at[:, span], acts.at[:, span], load_sem.at[2 + piece])
+
+    for piece in range(len(widths)):
+        load(piece).start()
 
     barrier = pltpu.get_barrier_semaphore()
     for link in ("x", "y", "in"):
@@ -216,25 +225,24 @@
             if events[k][step]:
                 pl.when(end == k)(act)
 
-    chunk = min(1024, tokens)
     group = BATCH * rows
-    dims = (((1,), (1,)), ((), ()))
+    def turn(piece):
+        load(piece).wait()
+        if piece == len(widths) - 1:
+            grads_t[...] = grads[...].T
+        else:
+            acts_t[piece * cut:(piece + 1) * cut, :] = acts[:, piece * cut:(piece + 1) * cut].T
 
     def multiply(batch, piece):
-        def body(i, carry):
-            cols = pl.ds(pl.multiple_of(i * chunk, chunk), chunk)
-            span = slice(batch * group, (batch + 1) * group)
-            if piece < len(widths) - 1:
-                left, right = slots_in[piece, span, :], acts[cols, piece * cut:(piece + 1) * cut]
-                term = lax.dot_general(left, right, dims, preferred_element_type=jnp.float32)
-                total[:, cols] = term if piece == 0 else total[:, cols] + term
-            else:
-                proj_out = lax.dot_general(slots_out[span, :], grads[cols, :], dims, preferred_element_type=jnp.float32)
-                joined = (total[:, cols] * proj_out).reshape(BATCH, rank, count, chunk)
-                parts[layer, batch, :, cols] = jnp.sum(joined, axis=1).reshape(BATCH * count, chunk)
-            return carry
-
-        lax.fori_loop(0, tokens // chunk, body, 0)
+        span = slice(batch * group, (batch + 1) * group)
+        if piece < len(widths) - 1:
+            right = acts_t[piece * cut:(piece + 1) * cut, :]
+            term = jnp.dot(slots_in[piece, span, :], right, preferred_element_type=jnp.float32)
+            total[...] = term if piece == 0 else total[...] + term
+        else:
+            proj_out = jnp.dot(slots_out[span, :], grads_t[...], preferred_element_type=jnp.float32)
+            joined = (total[...] * proj_out).reshape(BATCH, rank, count, tokens)
+            parts[layer, batch] = jnp.sum(joined, axis=1).reshape(BATCH * count, tokens)
 
     def share(batch, k, to):
         return pltpu.make_async_remote_copy(
@@ -263,9 +271,9 @@
 
     for step, (batch, piece) in enumerate(steps):
         communicate(step)
-        if step == 0:
-            load_acts.wait()
-            load_grads.wait()
+        if batch is None:
+            turn(piece)
+            continue
         multiply(batch, piece)
         if piece == 0 and batch > 0:
             finish(batch - 1)
@@ -299,7 +307,7 @@
     return pl.pallas_call(
         functools.partial(kernel, nz, layers, count, rank, widths),
         out_shape=jax.ShapeDtypeStruct((slots * count, tokens), jnp.float32),
-        in_specs=[pl.BlockSpec(memory_space=pl.ANY)] * 4,
+        in_specs=[pl.BlockSpec(memory_space=pltpu.HBM)] * 4,
         out_specs=pl.BlockSpec(memory_space=pltpu.VMEM),
         scratch_shapes=[
             pltpu.VMEM((count, rank, d_in), jnp.bfloat16),
@@ -308,18 +316,20 @@
             pltpu.VMEM((slots * rows, d_out), jnp.bfloat16),
             pltpu.VMEM((tokens, d_in), jnp.bfloat16),
             pltpu.VMEM((tokens, d_out), jnp.bfloat16),
+            pltpu.VMEM((d_in, tokens), jnp.bfloat16),
+            pltpu.VMEM((d_out, tokens), jnp.bfloat16),
             pltpu.VMEM((BATCH * rows, tokens), jnp.float32),
             pltpu.VMEM((layers, slots // BATCH, BATCH * count, tokens), jnp.float32),
-            dma((4,)),
+            dma((CUTS + 3,)),
             dma((slots, CUTS + 1)),
             dma((4, queue)),
             dma((slots // BATCH, layers)),
             dma((slots // BATCH, layers)),
         ],
         compiler_params=pltpu.CompilerParams(
-            collective_id=0, has_side_effects=True, vmem_limit_bytes=60 * 1024 * 1024
+            collective_id=0, has_side_effects=True, vmem_limit_bytes=LIMIT * 1024 * 1024
         ),
-    )(input_factors[:, 0], output_factors[:, 0], layer_inputs[0], output_grads[0])
+    )(*[pltpu.with_memory_space_constraint(a, pltpu.HBM) for a in (input_factors[:, 0], output_factors[:, 0], layer_inputs[0], output_grads[0])])
 
 
 def solution(mesh):

time: 43.9 us -> 41 us (0.934)
  Pallas kernels: 41.9 us -> 40.1 us
  local copies, waits for them, and re-layouts: 1.89 us -> 0.8 us
    pallas_call x1, Pallas kernels: 41.9 us -> 40.1 us  [shards(): pl.pallas_call(functools.partial(kernel, nz, layers, count, rank, widths)...]
    unnamed x1, local copies, waits for them, and re-layouts: 1.89 us -> 0.8 us
where the time goes in v3:
time: 41 us; the launch traced here: 40.9 us
  Pallas kernels  40.1 us (98%)
  local copies, waits for them, and re-layouts  0.8 us (2%)
    pallas_call x1, Pallas kernels, shards(): pl.pallas_call(functools.partial(kernel, nz, layers, count, rank, widths)...  40.1 us

profile of v3, /device:TPU:0, one launch (start us, length us, event | category | flops | bytes accessed | tf_op | source)
XLA Modules:
  0.0 40.9 jit_solution(592701739581562134)
XLA Ops:
  0.0 40.1 %shard_map.46 = f32[128,1024]{1,0:T(8,128)S(1)} custom-call(bf16[8,4,4096]{2,1,0:T(4,128)(2,1)} %bitcast.6, bf16[8,4,512]{2,1,0:T(4,128)(2,1)} %bitcast.7, bf16[1024,4096]{1,0:T(8,128)(2,1)} %bitcast.4, bf16[1024,512]{1,0:T(8,128)(2,1)} %bitcast.5), custom_call_target="tpu_custom_call" | custom-call | tf_op jit(solution)/shard_map/pallas_call | solution.py:307
  40.1 0.8 %copy.6 = f32[128,1024]{1,0:T(8,128)} copy(f32[128,1024]{1,0:T(8,128)S(1)} %shard_map.46) | data formatting | bytes 1048576

commit v4 on v3

--- a/solution.py
+++ b/solution.py
@@ -21,11 +21,11 @@
 BEGIN = 2.5
 TUNED = {
     4: {
-        (0, "x"): ((ACROSS_Y, 0), (OWN, 2), (OWN, 0), (ACROSS_Y, 2), (OWN, 1), (OWN, 3)),
+        (0, "x"): ((OWN, 2), (ACROSS_Y, 2), (ACROSS_Y, 0), (OWN, 0), (OWN, 1), (OWN, 3)),
         (0, "in"): ((OWN, 0), (DIAG, 2), (DIAG, 0)),
-        (1, "x"): ((ACROSS_Y, 1), (OWN, 3), (OWN, 1), (OWN, 0), (ACROSS_Y, 3), (OWN, 2)),
+        (1, "x"): ((OWN, 3), (OWN, 1), (ACROSS_Y, 3), (ACROSS_Y, 1), (OWN, 2), (OWN, 0)),
         (1, "in"): ((OWN, 1), (OWN, 0)),
-        (1, "ex"): ((OWN, 2), (OWN, 3), (DIAG, 1), (OWN, 1), (DIAG, 3)),
+        (1, "ex"): ((OWN, 1), (OWN, 2), (DIAG, 1), (OWN, 3), (DIAG, 3)),
     }
 }
 

time: 41 us -> 40.4 us (0.985)
  Pallas kernels: 40.1 us -> 39.5 us
    pallas_call x1, Pallas kernels: 40.1 us -> 39.5 us  [shards(): pl.pallas_call(functools.partial(kernel, nz, layers, count, rank, widths)...]
where the time goes in v4:
time: 40.4 us; the launch traced here: 40.3 us
  Pallas kernels  39.5 us (98%)
  local copies, waits for them, and re-layouts  0.8 us (2%)
    pallas_call x1, Pallas kernels, shards(): pl.pallas_call(functools.partial(kernel, nz, layers, count, rank, widths)...  39.5 us

profile of v4, /device:TPU:0, one launch (start us, length us, event | category | flops | bytes accessed | tf_op | source)
XLA Modules:
  0.0 40.3 jit_solution(2503486866757062807)
XLA Ops:
  0.0 39.5 %shard_map.46 = f32[128,1024]{1,0:T(8,128)S(1)} custom-call(bf16[8,4,4096]{2,1,0:T(4,128)(2,1)} %bitcast.6, bf16[8,4,512]{2,1,0:T(4,128)(2,1)} %bitcast.7, bf16[1024,4096]{1,0:T(8,128)(2,1)} %bitcast.4, bf16[1024,512]{1,0:T(8,128)(2,1)} %bitcast.5), custom_call_target="tpu_custom_call" | custom-call | tf_op jit(solution)/shard_map/pallas_call | solution.py:307
  39.5 0.8 %copy.6 = f32[128,1024]{1,0:T(8,128)} copy(f32[128,1024]{1,0:T(8,128)S(1)} %shard_map.46) | data formatting | bytes 1048576

commit v5 on v4

--- a/solution.py
+++ b/solution.py
@@ -14,6 +14,7 @@
 LIMIT = 48
 BATCH = 4
 AHEAD = 2
+PARTS = 1
 LATENCY = 1.6
 RATE = 730.0
 COMPUTE = 0.5
@@ -164,8 +165,6 @@
         span = pl.ds(piece * cut, cut)
         return pltpu.make_async_copy(acts_hbm.at[:, span], acts.at[:, span], load_sem.at[2 + piece])
 
-    for piece in range(len(widths)):
-        load(piece).start()
 
     barrier = pltpu.get_barrier_semaphore()
     for link in ("x", "y", "in"):
@@ -177,6 +176,8 @@
     def _():
         pl.semaphore_signal(barrier, inc=1, device_id=target["ex"], device_id_type=MESH)
 
+    for piece in range(len(widths)):
+        load(piece).start()
     load_in.wait()
     load_out.wait()
     for piece in range(len(widths) - 1):
@@ -295,6 +296,17 @@
             share(batch, k, layer).wait_send()
 
 
+def store(scores_ref, out_ref, sem):
+    rows = scores_ref.shape[0] // PARTS
+    copies = []
+    for part in range(PARTS):
+        span = pl.ds(part * rows, rows)
+        copies.append(pltpu.make_async_copy(scores_ref.at[span, :], out_ref.at[span, :], sem.at[part]))
+        copies[-1].start()
+    for copy in copies:
+        copy.wait()
+
+
 def shards(nz, layers, layer_inputs, output_grads, input_factors, output_factors):
     count, _, rank, d_in = input_factors.shape
     d_out = output_factors.shape[3]
@@ -304,7 +316,7 @@
     slots = 4 * nz
     queue = max(len(items) for items in simulate(nz, widths)[0].values())
     dma = pltpu.SemaphoreType.DMA
-    return pl.pallas_call(
+    scores = pl.pallas_call(
         functools.partial(kernel, nz, layers, count, rank, widths),
         out_shape=jax.ShapeDtypeStruct((slots * count, tokens), jnp.float32),
         in_specs=[pl.BlockSpec(memory_space=pltpu.HBM)] * 4,
@@ -330,6 +342,14 @@
             collective_id=0, has_side_effects=True, vmem_limit_bytes=LIMIT * 1024 * 1024
         ),
     )(*[pltpu.with_memory_space_constraint(a, pltpu.HBM) for a in (input_factors[:, 0], output_factors[:, 0], layer_inputs[0], output_grads[0])])
+    return pl.pallas_call(
+        store,
+        out_shape=jax.ShapeDtypeStruct(scores.shape, scores.dtype),
+        in_specs=[pl.BlockSpec(memory_space=pltpu.VMEM)],
+        out_specs=pl.BlockSpec(memory_space=pltpu.HBM),
+        scratch_shapes=[dma((PARTS,))],
+        compiler_params=pltpu.CompilerParams(vmem_limit_bytes=8 * 1024 * 1024),
+    )(scores)
 
 
 def solution(mesh):

time: 40.4 us -> 40.4 us (level)
  local copies, waits for them, and re-layouts: 0.8 us -> 0 us
  Pallas kernels: 39.5 us -> 40.3 us
    pallas_call x0 -> x1, Pallas kernels: none -> 0.8 us  [shards(): pl.pallas_call(store, out_shape=jax.ShapeDtypeStruct(scores.shape, scores...]
    unnamed x1 -> x0, local copies, waits for them, and re-layouts: 0.8 us -> none
where the time goes in v5:
time: 40.4 us; the launch traced here: 40.3 us
  Pallas kernels  40.3 us (100%)
    pallas_call x1, Pallas kernels, shards(): pl.pallas_call(functools.partial(kernel, nz, layers, count, rank, widths)...  39.5 us

profile of v5, /device:TPU:0, one launch (start us, length us, event | category | flops | bytes accessed | tf_op | source)
XLA Modules:
  0.0 40.3 jit_solution(8759246793241988494)
XLA Ops:
  0.0 39.5 %shard_map.46.scores_ref = f32[128,1024]{1,0:T(8,128)S(1)} custom-call(bf16[8,4,4096]{2,1,0:T(4,128)(2,1)} %bitcast.6, bf16[8,4,512]{2,1,0:T(4,128)(2,1)} %bitcast.7, bf16[1024,4096]{1,0:T(8,128)(2,1)} %bitcast.4, bf16[1024,512]{1,0:T(8,128)(2,1)} %bitcast.5), custom_call_target="tpu_custom_call" | custom-call | tf_op jit(solution)/shard_map/pallas_call | solution.py:319
  39.5 0.8 %shard_map.47 = f32[128,1024]{1,0:T(8,128)} custom-call(f32[128,1024]{1,0:T(8,128)S(1)} %shard_map.46.scores_ref), custom_call_target="tpu_custom_call" | custom-call | tf_op jit(solution)/shard_map/pallas_call | solution.py:345
